TPU v7x, 32 devices: a whole 2x2x4 slice. The times are simulated.
32 devices in a mesh: sector: 4 (over y, x), term: 8 (over z, core).
Axes of the slice: x: 2, y: 2, z: 4, core: 2. Of those that a mesh axis runs over, the one named last changes fastest.
Arguments:
- wavefunction: bfloat16 [256, 4, 2, 256], P('term', 'sector'), may hold values from -6 to 6
- left_ops: bfloat16 [128, 4, 256, 256], P('term', 'sector'), may hold values from -0.5 to 0.5
- right_ops: bfloat16 [128, 4, 256, 256], P('term', 'sector'), may hold values from -0.03125 to 0.03125
- op_scales: float32 [128, 4], P('term', 'sector'), may hold values from 0.5 to 2
- sources: int32 [128, 4], P('term', 'sector'), may hold values from 0 to 1
- coupled_sectors: int32 [4, 2], P('sector'), may hold values from 0 to 3, as said below
- left_dims: int32 [4], replicated, may hold values from 1 to 256, 768 in all
- right_dims: int32 [4], replicated, may hold values from 1 to 256, 768 in all
Outputs:
- sigma: bfloat16 [256, 4, 2, 256], P('term', 'sector')
Inputs may be any that keep to these rules, and one draw needn't show every extreme that they name: `coupled_sectors`: the 2 sectors of each row are distinct. `left_dims`: the sizes of all sectors add up to 768. `right_dims`: the sizes of all sectors add up to 768.
All inputs are finite; a program needn't handle non-finite values.
Results may differ from a plain program's by a relative error of at most 0.025.
Values may be sent and summed in bfloat16 or wider, within the bound.
No kernel may reach another device: no remote copies, remote signals or barrier semaphores. Data moves between devices by JAX's collectives and lax.ppermute only.
A program may use at most 64 MiB of HBM per device.

v0:
```python
import functools

import jax
import jax.numpy as jnp
from jax import lax
from jax.experimental import pallas as pl
from jax.experimental.pallas import tpu as pltpu
from jax.sharding import PartitionSpec as P


VMEM = pltpu.VMEM
SMEM = pltpu.SMEM
GROUPS = (((0, 0), (0, 1)), ((1, 0), (2, 0), (3, 0), (3, 1)), ((1, 1), (2, 1)))


def swap(x, axis, size, mask):
    return lax.ppermute(x, axis, [(i, i ^ mask) for i in range(size)])


def along(x, size, by):
    pairs = [(i, (i + 2 * by) % size) for i in range(size)]
    return lax.ppermute(x, "term", pairs)


def load_kernel(sectors, coupled_ref, left_ref, right_ref, wave_ref, ops_ref, coops_ref, scale_ref, source_ref,
                ops_out, coops_out, scale_out, source_out, own_out, masks_out, live_out, wave_vmem, sems):
    copies = [pltpu.make_async_copy(src, dst, sems.at[n]) for n, (src, dst) in enumerate((
        (wave_ref, wave_vmem), (ops_ref, ops_out), (coops_ref, coops_out),
        (scale_ref, scale_out), (source_ref, source_out)))]
    for copy in copies:
        copy.start()
    chosen, vectors, rows, states = own_out.shape
    me, first_row = lax.axis_index("sector"), lax.axis_index("term") * rows
    row = lax.broadcasted_iota(jnp.int32, (rows, states), 0) + first_row
    col = lax.broadcasted_iota(jnp.int32, (rows, states), 1)
    live_out[...] = ((row < left_ref[me]) & (col < right_ref[me])).astype(jnp.float32)
    for c in range(chosen):
        sector = coupled_ref[0, c]
        live = ((row < left_ref[sector]) & (col < right_ref[sector])).astype(jnp.float32)
        for m in range(sectors):
            masks_out[c, m] = jnp.where((sector ^ me) == m, live, 0.0)
    copies[0].wait()
    for v in range(vectors):
        value = wave_vmem[:, 0, v, :].astype(jnp.float32)
        for c in range(chosen):
            own_out[c, v] = masks_out[c, 0] * value
    for copy in copies[1:]:
        copy.wait()


def pick_kernel(masks_ref, own_ref, *refs):
    blocks, out_ref = refs[:-1], refs[-1]
    chosen, vectors = out_ref.shape[:2]
    for v in range(vectors):
        values = [block[:, 0, v, :].astype(jnp.float32) for block in blocks]
        for c in range(chosen):
            total = own_ref[c, v]
            for m, value in enumerate(values):
                total = total + masks_ref[c, m + 1] * value
            out_ref[c, v] = total.astype(out_ref.dtype)


def contract(scale_ref, source_ref, left_ref, right_ref, psi_ref, prod_ref):
    terms, _, states, _ = left_ref.shape
    vectors = psi_ref.shape[2] // states
    for t in range(terms):
        prod = jnp.dot(left_ref[t, 0], psi_ref[source_ref[t]], preferred_element_type=jnp.float32)
        prod = (prod * scale_ref[t]).astype(jnp.bfloat16)
        for v in range(vectors):
            prod_ref[v * states:(v + 1) * states, t * states:(t + 1) * states] = (
                prod[:, v * states:(v + 1) * states])
    return jnp.dot(prod_ref[...], right_ref[...].reshape(terms * states, states),
                   preferred_element_type=jnp.float32)


def project(coops_ref, scale_ref, source_ref, blocks, places, stack_ref, prod_ref):
    chosen, vectors, rows, states = blocks[0].shape
    for n, block in enumerate(blocks):
        for c in range(chosen):
            for v in range(vectors):
                at = (n * vectors + v) * rows
                stack_ref[c, at:at + rows] = block[c, v]
    used = len(blocks) * vectors * rows
    for t in range(coops_ref.shape[0]):
        prod = jnp.dot(stack_ref[source_ref[t], :used], coops_ref[t, 0], preferred_element_type=jnp.float32)
        prod = (prod * scale_ref[t]).astype(prod_ref.dtype)
        for n, place in enumerate(places):
            start = pl.multiple_of(place * rows, rows)
            for v in range(vectors):
                at = (n * vectors + v) * rows
                prod_ref[t, pl.ds(start, rows), v * states:(v + 1) * states] = prod[at:at + rows]


def owners(kinds):
    return [lax.axis_index("term") ^ (2 * away + other) for away, other in kinds]


def apply_left(ops_ref, prod_ref, core, out_ref):
    chips, vectors, rows, states = out_ref.shape
    total = None
    for t in range(ops_ref.shape[0]):
        left = jnp.concatenate(
            [ops_ref[t, 0, pl.ds(pl.multiple_of((2 * z + core) * rows, rows), rows), :] for z in range(chips)])
        part = jnp.dot(left, prod_ref[t], preferred_element_type=jnp.float32)
        total = part if total is None else total + part
    for z in range(chips):
        for v in range(vectors):
            out_ref[z, v] = total[z * rows:(z + 1) * rows, v * states:(v + 1) * states].astype(out_ref.dtype)


def first_kernel(kinds, scale_ref, source_ref, coops_ref, *refs):
    blocks, prod_ref, stack_ref = refs[:-2], refs[-2], refs[-1]
    project(coops_ref, scale_ref, source_ref, blocks, owners(kinds), stack_ref, prod_ref)


def more_kernel(kinds, scale_ref, source_ref, coops_ref, prod_in, *refs):
    blocks, prod_ref, stack_ref = refs[:-2], refs[-2], refs[-1]
    project(coops_ref, scale_ref, source_ref, blocks, owners(kinds), stack_ref, prod_ref)


def second_kernel(kinds, scale_ref, source_ref, coops_ref, ops_ref, prod_in, *refs):
    blocks, prod_ref, send_ref, stack_ref = refs[:-3], refs[-3], refs[-2], refs[-1]
    project(coops_ref, scale_ref, source_ref, blocks, owners(kinds), stack_ref, prod_ref)
    apply_left(ops_ref, prod_ref, 1 - (lax.axis_index("term") & 1), send_ref)


def third_kernel(ops_ref, prod_ref, keep_ref):
    apply_left(ops_ref, prod_ref, lax.axis_index("term") & 1, keep_ref)


def split_kernel(chips, keep_ref, recv_ref, *outs):
    chip = lax.axis_index("term") >> 1
    for n in range(chips):
        at = lax.rem(chip + n, chips)
        outs[n][...] = (keep_ref[at] + recv_ref[at].astype(jnp.float32)).astype(outs[n].dtype)


def call(kernel, outs, smem, vmem, args, scratch=(), aliases={}):
    args = [pltpu.with_memory_space_constraint(x, SMEM if n < smem else VMEM) for n, x in enumerate(args)]
    return pl.pallas_call(
        kernel,
        out_shape=outs,
        in_specs=[pl.BlockSpec(memory_space=SMEM)] * smem + [pl.BlockSpec(memory_space=VMEM)] * vmem,
        out_specs=jax.tree.map(lambda _: pl.BlockSpec(memory_space=VMEM), outs),
        scratch_shapes=list(scratch),
        input_output_aliases=aliases,
        compiler_params=pltpu.CompilerParams(vmem_limit_bytes=24 << 20),
    )(*args)


def final_kernel(live_ref, total_ref, *refs):
    parts, out_ref = refs[:-1], refs[-1]
    for v in range(total_ref.shape[0]):
        total = total_ref[v]
        for part in parts:
            total = total + part[v].astype(jnp.float32)
        out_ref[:, 0, v, :] = (live_ref[...] * total).astype(out_ref.dtype)


def direct(wave, left_ops, right_ops, op_scales, sources, coupled, left_dims, right_dims):
    sectors, term_devices = lax.axis_size("sector"), lax.axis_size("term")
    chips = term_devices // 2
    rows, _, vectors, states = wave.shape
    terms, chosen = left_ops.shape[0], coupled.shape[1]
    bf16, f32 = jnp.bfloat16, jnp.float32

    any_spec, smem_spec = pl.BlockSpec(memory_space=pl.ANY), pl.BlockSpec(memory_space=SMEM)
    vmem_spec = pl.BlockSpec(memory_space=VMEM)
    hbm = lambda x: pltpu.with_memory_space_constraint(x, pltpu.HBM)
    shares = [swap(wave, "sector", sectors, m) for m in range(1, sectors)]
    ops, coops, scales, picks, mine, masks, live = pl.pallas_call(
        functools.partial(load_kernel, sectors),
        out_shape=(VMEM(left_ops.shape, bf16), VMEM(right_ops.shape, bf16), SMEM((terms,), f32),
                   SMEM((terms,), jnp.int32), VMEM((chosen, vectors, rows, states), f32),
                   VMEM((chosen, sectors, rows, states), f32), VMEM((rows, states), f32)),
        in_specs=[smem_spec] * 3 + [any_spec] * 5,
        out_specs=(vmem_spec, vmem_spec, smem_spec, smem_spec, vmem_spec, vmem_spec, vmem_spec),
        scratch_shapes=[VMEM(wave.shape, bf16), pltpu.SemaphoreType.DMA((5,))],
        compiler_params=pltpu.CompilerParams(vmem_limit_bytes=4 << 20),
    )(hbm(coupled), hbm(left_dims), hbm(right_dims), hbm(wave), hbm(left_ops), hbm(right_ops),
      hbm(op_scales.reshape(-1)), hbm(sources.reshape(-1)))
    own = call(pick_kernel, VMEM((chosen, vectors, rows, states), bf16), 0, 1 + sectors,
               (masks, mine, *shares))
    line = [own] + [swap(own, "term", term_devices, 2 * m) for m in range(1, chips)]
    pair = [swap(b, "term", term_devices, 1) for b in line]
    prod_shape = VMEM((terms, states, vectors * states), bf16)
    piece = (chips, vectors, rows, states)
    blocks = {(n, o): (pair if o else line)[n] for n in range(chips) for o in range(2)}
    stack = lambda kinds: (VMEM((chosen, len(kinds) * vectors * rows, states), bf16),)
    prod = None
    for kinds in GROUPS[:-1]:
        given = [blocks[kind] for kind in kinds]
        if prod is None:
            prod = call(functools.partial(first_kernel, kinds), prod_shape, 2, 1 + len(kinds),
                        (scales, picks, coops, *given), stack(kinds))
        else:
            prod = call(functools.partial(more_kernel, kinds), prod_shape, 2, 2 + len(kinds),
                        (scales, picks, coops, prod, *given), stack(kinds), {3: 0})
    kinds = GROUPS[-1]
    prod, send = call(functools.partial(second_kernel, kinds), (prod_shape, VMEM(piece, bf16)), 2, 3 + len(kinds),
                      (scales, picks, coops, ops, prod, *[blocks[kind] for kind in kinds]), stack(kinds), {4: 0})
    keep = call(third_kernel, VMEM(piece, f32), 0, 2, (ops, prod))
    parts = call(functools.partial(split_kernel, chips),
                 (VMEM((vectors, rows, states), f32),)
                 + (VMEM((vectors, rows, states), bf16),) * (chips - 1),
                 0, 2, (keep, swap(send, "term", term_devices, 1)))
    others = [along(parts[m], term_devices, m) for m in range(1, chips)]
    return call(final_kernel, jax.ShapeDtypeStruct(wave.shape, bf16), 0, 1 + chips,
                (live, parts[0], *others))


def whole_kernel(scale_ref, source_ref, left_ref, right_ref, blocks_ref, out_ref, prod_ref):
    out_ref[...] = contract(scale_ref, source_ref, left_ref, right_ref, blocks_ref, prod_ref)


def gathered(wave, left_ops, right_ops, op_scales, sources, coupled, left_dims, right_dims):
    rows, _, vectors, states = wave.shape
    terms, chosen = left_ops.shape[0], coupled.shape[1]
    me, place = lax.axis_index("sector"), lax.axis_index("term")
    shares = lax.all_gather(wave[:, 0], "sector", axis=0)
    picks = coupled[0]
    row = lax.broadcasted_iota(jnp.int32, (1, rows, 1, states), 1) + place * rows
    col = lax.broadcasted_iota(jnp.int32, (1, rows, 1, states), 3)
    live = ((row < jnp.take(left_dims, picks)[:, None, None, None])
            & (col < jnp.take(right_dims, picks)[:, None, None, None]))
    own = jnp.where(live, jnp.take(shares, picks, axis=0), jnp.zeros((), wave.dtype))
    blocks = lax.all_gather(own, "term", axis=1, tiled=True).reshape(chosen, -1, vectors * states)
    total = call(whole_kernel, jax.ShapeDtypeStruct((vectors * states, states), jnp.float32),
                 2, 3, (op_scales.reshape(-1), sources.reshape(-1), left_ops, right_ops, blocks),
                 (VMEM((vectors * states, terms * states), jnp.bfloat16),))
    total = jnp.transpose(total.reshape(vectors, states, states), (1, 0, 2))
    row = lax.broadcasted_iota(jnp.int32, total.shape, 0)
    col = lax.broadcasted_iota(jnp.int32, total.shape, 2)
    total = jnp.where((row < left_dims[me]) & (col < right_dims[me]), total, 0.0)
    return lax.psum_scatter(total.astype(jnp.bfloat16), "term", scatter_dimension=0, tiled=True)[:, None]


def solution(mesh):
    in_specs = (
        P("term", "sector", None, None),
        P("term", "sector", None, None),
        P("term", "sector", None, None),
        P("term", "sector"),
        P("term", "sector"),
        P("sector", None),
        P(),
        P(),
    )
    out_specs = P("term", "sector", None, None)
    small = mesh.shape["sector"] == 4 and mesh.shape["term"] == 8

    def local(*args):
        return (direct if small else gathered)(*args)

    return jax.shard_map(local, mesh=mesh, in_specs=in_specs, out_specs=out_specs, check_vma=False)
```

profile of v0, /device:TPU:0, one launch (start us, length us, event | category | flops | bytes accessed | tf_op | source)
XLA Modules:
  0.0 30.4 jit_solution(17953773262345843396)
XLA Ops:
  0.0 3.0 %collective-permute-start = (bf16[32,1,2,256]{3,2,1,0:T(2,128)(2,1)}, bf16[32,1,2,256]{3,2,1,0:T(2,128)(2,1)S(1)}, u32[]{:S(2)}, u32[]{:S(2)}) collective-permute-start(bf16[32,1,2,256]{3,2,1,0:T(2,128)(2,1)} %wave_ref.1), channel_id=1, source_target_pairs={{0,8},{8,0},{16,24},{24,16},{1,9},{9,1},{17,25},{25,17},{2,10},{10... | collective-permute-start | bytes 98312 | tf_op jit(solution)/shard_map/ppermute | solution.py:17
  3.0 1.5 %collective-permute-start.1 = (bf16[32,1,2,256]{3,2,1,0:T(2,128)(2,1)}, bf16[32,1,2,256]{3,2,1,0:T(2,128)(2,1)S(1)}, u32[]{:S(2)}, u32[]{:S(2)}) collective-permute-start(bf16[32,1,2,256]{3,2,1,0:T(2,128)(2,1)} %wave_ref.1), channel_id=1, source_target_pairs={{0,16},{8,24},{16,0},{24,8},{1,17},{9,25},{17,1},{25,9},{2,18},{10... | collective-permute-start | bytes 98312 | tf_op jit(solution)/shard_map/ppermute | solution.py:17
  4.5 3.0 %shard_map.82 = (bf16[16,1,256,256]{3,2,1,0:T(8,128)(2,1)S(1)}, bf16[16,1,256,256]{3,2,1,0:T(8,128)(2,1)S(1)}, f32[16]{0:T(128)S(4)}, s32[16]{0:T(128)S(4)}, f32...) custom-call(s32[1,2]{1,0:T(1,128)} %coupled_ref.1, s32[4]{0:T(128)} %left_ref.1, ...), custom_call_target="tpu_custom_call" | custom-call | tf_op jit(solution)/shard_map/pallas_call | solution.py:171
  7.5 0.0 collective-permute-done.1.refs_1_
  7.5 2.0 %collective-permute-done.2.refs_2_ = bf16[32,1,2,256]{3,2,1,0:T(2,128)(2,1)S(1)} collective-permute-done((bf16[32,1,2,256]{3,2,1,0:T(2,128)(2,1)}, bf16[32,1,2,256]{3,2,1,0:T(2,128)(2,1)S(1)}, u32[]{:S(2)}, u32[]{:S(2)}) %collective-permute-start.2) | collective-permute-done | bytes 32800 | tf_op jit(solution)/shard_map/ppermute | solution.py:17
  9.5 0.1 shard_map.83.refs_0_
  9.7 3.7 %collective-permute-start.6 = (bf16[2,2,32,256]{3,2,1,0:T(8,128)(2,1)S(1)}, bf16[2,2,32,256]{3,2,1,0:T(8,128)(2,1)S(1)}, u32[]{:S(2)}, u32[]{:S(2)}) collective-permute-start(bf16[2,2,32,256]{3,2,1,0:T(8,128)(2,1)S(1)} %shard_map.83.refs_0_), channel_id=1, source_target_pairs={{0,6},{1,7},{2,4},{3,5},{4,2},{5,3},{6,0},{7,1},{8,14},{9,15},{10,... | collective-permute-start | bytes 196616 | tf_op jit(solution)/shard_map/ppermute | solution.py:17
  13.3 0.8 %collective-permute-start.5 = (bf16[2,2,32,256]{3,2,1,0:T(8,128)(2,1)S(1)}, bf16[2,2,32,256]{3,2,1,0:T(8,128)(2,1)S(1)}, u32[]{:S(2)}, u32[]{:S(2)}) collective-permute-start(bf16[2,2,32,256]{3,2,1,0:T(8,128)(2,1)S(1)} %shard_map.83.refs_0_), channel_id=1, source_target_pairs={{0,4},{1,5},{2,6},{3,7},{4,0},{5,1},{6,2},{7,3},{8,12},{9,13},{10,... | collective-permute-start | bytes 196616 | tf_op jit(solution)/shard_map/ppermute | solution.py:17
  14.1 1.8 %collective-permute-done.6.refs_2_ = bf16[2,2,32,256]{3,2,1,0:T(8,128)(2,1)S(1)} collective-permute-done((bf16[2,2,32,256]{3,2,1,0:T(8,128)(2,1)S(1)}, bf16[2,2,32,256]{3,2,1,0:T(8,128)(2,1)S(1)}, u32[]{:S(2)}, u32[]{:S(2)}) %collective-permute-start.6) | collective-permute-done | bytes 65568 | tf_op jit(solution)/shard_map/ppermute | solution.py:17
  15.9 1.7 %collective-permute-done.4.refs_0_ = bf16[2,2,32,256]{3,2,1,0:T(8,128)(2,1)S(1)} collective-permute-done((bf16[2,2,32,256]{3,2,1,0:T(8,128)(2,1)S(1)}, bf16[2,2,32,256]{3,2,1,0:T(8,128)(2,1)S(1)}, u32[]{:S(2)}, u32[]{:S(2)}) %collective-permute-start.4) | collective-permute-done | bytes 65568 | tf_op jit(solution)/shard_map/ppermute | solution.py:17
  17.6 0.9 %collective-permute-done.5.refs_1_ = bf16[2,2,32,256]{3,2,1,0:T(8,128)(2,1)S(1)} collective-permute-done((bf16[2,2,32,256]{3,2,1,0:T(8,128)(2,1)S(1)}, bf16[2,2,32,256]{3,2,1,0:T(8,128)(2,1)S(1)}, u32[]{:S(2)}, u32[]{:S(2)}) %collective-permute-start.5) | collective-permute-done | bytes 65568 | tf_op jit(solution)/shard_map/ppermute | solution.py:17
  18.5 0.5 %shard_map.84.prod_in = bf16[16,256,512]{2,1,0:T(8,128)(2,1)S(1)} custom-call(f32[16]{0:T(128)S(4)} %get-tuple-element.20.scale_ref, s32[16]{0:T(128)S(4)} %get-tuple-element.21.source_ref, bf16[16,1,256,256]{3,2,1,0:T(8,128)(2,1)S(1)} %get-tuple-element.22.coops_ref, bf16[2,2,32,256]{3,2,1,0:T(8,128)(2,1)S(1)} %shard_map.83.refs_0_, ...), custom_call_target="tpu_custom_call" | custom-call | tf_op jit(solution)/shard_map/pallas_call | solution.py:140
  19.0 0.7 %shard_map.85.prod_in = bf16[16,256,512]{2,1,0:T(8,128)(2,1)S(1)} custom-call(f32[16]{0:T(128)S(4)} %get-tuple-element.20.scale_ref, s32[16]{0:T(128)S(4)} %get-tuple-element.21.source_ref, bf16[16,1,256,256]{3,2,1,0:T(8,128)(2,1)S(1)} %get-tuple-element.22.coops_ref, bf16[16,256,512]{2,1,0:T(8,128)(2,1)S(1)} %shard_map.84.prod_in, ...), custom_call_target="tpu_custom_call", output_to_operand_aliasing={{}: (3, {})} | custom-call | tf_op jit(solution)/shard_map/pallas_call | solution.py:140
  19.7 0.0 collective-permute-done.9.refs_1_
  19.7 1.2 %shard_map.86 = (bf16[16,256,512]{2,1,0:T(8,128)(2,1)S(1)}, bf16[4,2,32,256]{3,2,1,0:T(8,128)(2,1)S(1)}) custom-call(f32[16]{0:T(128)S(4)} %get-tuple-element.20.scale_ref, s32[16]{0:T(128)S(4)} %get-tuple-element.21.source_ref, bf16[16,1,256,256]{3,2,1,0:T(8,128)(2,1)S(1)} %get-tuple-element.22.coops_ref, ...), custom_call_target="tpu_custom_call", output_to_operand_aliasing={{0}: (4, {})} | custom-call | tf_op jit(solution)/shard_map/pallas_call | solution.py:140
  20.9 0.6 %collective-permute-start.10 = (bf16[4,2,32,256]{3,2,1,0:T(8,128)(2,1)S(1)}, bf16[4,2,32,256]{3,2,1,0:T(8,128)(2,1)S(1)}, u32[]{:S(2)}, u32[]{:S(2)}) collective-permute-start(bf16[4,2,32,256]{3,2,1,0:T(8,128)(2,1)S(1)} %get-tuple-element.26), channel_id=1, source_target_pairs={{0,1},{1,0},{2,3},{3,2},{4,5},{5,4},{6,7},{7,6},{8,9},{9,8},{10,11... | collective-permute-start | bytes 393224 | tf_op jit(solution)/shard_map/ppermute | solution.py:17
  21.5 0.7 %shard_map.87.keep_ref = f32[4,2,32,256]{3,2,1,0:T(8,128)S(1)} custom-call(bf16[16,1,256,256]{3,2,1,0:T(8,128)(2,1)S(1)} %get-tuple-element.19.ops_ref, bf16[16,256,512]{2,1,0:T(8,128)(2,1)S(1)} %get-tuple-element.25.prod_ref), custom_call_target="tpu_custom_call" | custom-call | tf_op jit(solution)/shard_map/pallas_call | solution.py:140
  22.2 0.3 collective-permute-done.10.recv_ref
  22.5 2.1 %collective-permute-start.11 = (bf16[2,32,256]{2,1,0:T(8,128)(2,1)S(1)}, bf16[2,32,256]{2,1,0:T(8,128)(2,1)S(1)}, u32[]{:S(2)}, u32[]{:S(2)}) collective-permute-start(bf16[2,32,256]{2,1,0:T(8,128)(2,1)S(1)} %get-tuple-element.28), channel_id=1, source_target_pairs={{0,2},{1,3},{2,4},{3,5},{4,6},{5,7},{6,0},{7,1},{8,10},{9,11},{10,... | collective-permute-start | bytes 98312 | tf_op jit(solution)/shard_map/ppermute | solution.py:22
  24.6 0.1 collective-permute-start.12
  24.7 2.3 %collective-permute-start.13 = (bf16[2,32,256]{2,1,0:T(8,128)(2,1)S(1)}, bf16[2,32,256]{2,1,0:T(8,128)(2,1)S(1)}, u32[]{:S(2)}, u32[]{:S(2)}) collective-permute-start(bf16[2,32,256]{2,1,0:T(8,128)(2,1)S(1)} %get-tuple-element.30), channel_id=1, source_target_pairs={{0,6},{1,7},{2,0},{3,1},{4,2},{5,3},{6,4},{7,5},{8,14},{9,15},{10,... | collective-permute-start | bytes 98312 | tf_op jit(solution)/shard_map/ppermute | solution.py:22
  27.0 1.6 %collective-permute-done.11.refs_0_ = bf16[2,32,256]{2,1,0:T(8,128)(2,1)S(1)} collective-permute-done((bf16[2,32,256]{2,1,0:T(8,128)(2,1)S(1)}, bf16[2,32,256]{2,1,0:T(8,128)(2,1)S(1)}, u32[]{:S(2)}, u32[]{:S(2)}) %collective-permute-start.11) | collective-permute-done | bytes 32800 | tf_op jit(solution)/shard_map/ppermute | solution.py:22
  28.6 1.1 %collective-permute-done.12.refs_1_ = bf16[2,32,256]{2,1,0:T(8,128)(2,1)S(1)} collective-permute-done((bf16[2,32,256]{2,1,0:T(8,128)(2,1)S(1)}, bf16[2,32,256]{2,1,0:T(8,128)(2,1)S(1)}, u32[]{:S(2)}, u32[]{:S(2)}) %collective-permute-start.12) | collective-permute-done | bytes 32800 | tf_op jit(solution)/shard_map/ppermute | solution.py:22
  29.7 0.7 %shard_map.89 = bf16[32,1,2,256]{3,2,1,0:T(2,128)(2,1)} custom-call(f32[32,256]{1,0:T(8,128)S(1)} %get-tuple-element.18.live_ref, f32[2,32,256]{2,1,0:T(8,128)S(1)} %get-tuple-element.27.total_ref, bf16[2,32,256]{2,1,0:T(8,128)(2,1)S(1)} %collective-permute-done.11.refs_0_, bf16[2,32,256]{2,1,0:T(8,128)(2,1)S(1)} %collective-permute-done.12.refs_1_, ...), custom_call_target="tpu_custom_call" | custom-call | tf_op jit(solution)/shard_map/pallas_call | solution.py:140
  (12 shorter events, 0.1 us)
Async XLA Ops:
  0.0 7.5 %collective-permute-start = (bf16[32,1,2,256]{3,2,1,0:T(2,128)(2,1)}, bf16[32,1,2,256]{3,2,1,0:T(2,128)(2,1)S(1)}, u32[]{:S(2)}, u32[]{:S(2)}) collective-permute-start(bf16[32,1,2,256]{3,2,1,0:T(2,128)(2,1)} %wave_ref.1), channel_id=1, source_target_pairs={{0,8},{8,0},{16,24},{24,16},{1,9},{9,1},{17,25},{25,17},{2,10},{10... | collective-permute-start | bytes 98312 | tf_op jit(solution)/shard_map/ppermute | solution.py:17
  3.0 4.5 %collective-permute-start.1 = (bf16[32,1,2,256]{3,2,1,0:T(2,128)(2,1)}, bf16[32,1,2,256]{3,2,1,0:T(2,128)(2,1)S(1)}, u32[]{:S(2)}, u32[]{:S(2)}) collective-permute-start(bf16[32,1,2,256]{3,2,1,0:T(2,128)(2,1)} %wave_ref.1), channel_id=1, source_target_pairs={{0,16},{8,24},{16,0},{24,8},{1,17},{9,25},{17,1},{25,9},{2,18},{10... | collective-permute-start | bytes 98312 | tf_op jit(solution)/shard_map/ppermute | solution.py:17
  4.5 5.0 %collective-permute-start.2 = (bf16[32,1,2,256]{3,2,1,0:T(2,128)(2,1)}, bf16[32,1,2,256]{3,2,1,0:T(2,128)(2,1)S(1)}, u32[]{:S(2)}, u32[]{:S(2)}) collective-permute-start(bf16[32,1,2,256]{3,2,1,0:T(2,128)(2,1)} %wave_ref.1), channel_id=1, source_target_pairs={{0,24},{8,16},{16,8},{24,0},{1,25},{9,17},{17,9},{25,1},{2,26},{10... | collective-permute-start | bytes 98312 | tf_op jit(solution)/shard_map/ppermute | solution.py:17
  9.7 6.2 %collective-permute-start.6 = (bf16[2,2,32,256]{3,2,1,0:T(8,128)(2,1)S(1)}, bf16[2,2,32,256]{3,2,1,0:T(8,128)(2,1)S(1)}, u32[]{:S(2)}, u32[]{:S(2)}) collective-permute-start(bf16[2,2,32,256]{3,2,1,0:T(8,128)(2,1)S(1)} %shard_map.83.refs_0_), channel_id=1, source_target_pairs={{0,6},{1,7},{2,4},{3,5},{4,2},{5,3},{6,0},{7,1},{8,14},{9,15},{10,... | collective-permute-start | bytes 196616 | tf_op jit(solution)/shard_map/ppermute | solution.py:17
  13.3 4.3 %collective-permute-start.4 = (bf16[2,2,32,256]{3,2,1,0:T(8,128)(2,1)S(1)}, bf16[2,2,32,256]{3,2,1,0:T(8,128)(2,1)S(1)}, u32[]{:S(2)}, u32[]{:S(2)}) collective-permute-start(bf16[2,2,32,256]{3,2,1,0:T(8,128)(2,1)S(1)} %shard_map.83.refs_0_), channel_id=1, source_target_pairs={{0,2},{1,3},{2,0},{3,1},{4,6},{5,7},{6,4},{7,5},{8,10},{9,11},{10,... | collective-permute-start | bytes 196616 | tf_op jit(solution)/shard_map/ppermute | solution.py:17
  13.3 5.2 %collective-permute-start.5 = (bf16[2,2,32,256]{3,2,1,0:T(8,128)(2,1)S(1)}, bf16[2,2,32,256]{3,2,1,0:T(8,128)(2,1)S(1)}, u32[]{:S(2)}, u32[]{:S(2)}) collective-permute-start(bf16[2,2,32,256]{3,2,1,0:T(8,128)(2,1)S(1)} %shard_map.83.refs_0_), channel_id=1, source_target_pairs={{0,4},{1,5},{2,6},{3,7},{4,0},{5,1},{6,2},{7,3},{8,12},{9,13},{10,... | collective-permute-start | bytes 196616 | tf_op jit(solution)/shard_map/ppermute | solution.py:17
  14.1 4.4 %collective-permute-start.3 = (bf16[2,2,32,256]{3,2,1,0:T(8,128)(2,1)S(1)}, bf16[2,2,32,256]{3,2,1,0:T(8,128)(2,1)S(1)}, u32[]{:S(2)}, u32[]{:S(2)}) collective-permute-start(bf16[2,2,32,256]{3,2,1,0:T(8,128)(2,1)S(1)} %shard_map.83.refs_0_), channel_id=1, source_target_pairs={{0,1},{1,0},{2,3},{3,2},{4,5},{5,4},{6,7},{7,6},{8,9},{9,8},{10,11... | collective-permute-start | bytes 196616 | tf_op jit(solution)/shard_map/ppermute | solution.py:17
  15.9 3.1 %collective-permute-start.7 = (bf16[2,2,32,256]{3,2,1,0:T(8,128)(2,1)S(1)}, bf16[2,2,32,256]{3,2,1,0:T(8,128)(2,1)S(1)}, u32[]{:S(2)}, u32[]{:S(2)}) collective-permute-start(bf16[2,2,32,256]{3,2,1,0:T(8,128)(2,1)S(1)} %collective-permute-done.6.refs_2_), channel_id=1, source_target_pairs={{0,1},{1,0},{2,3},{3,2},{4,5},{5,4},{6,7},{7,6},{8,9},{9,8},{10,11... | collective-permute-start | bytes 196616 | tf_op jit(solution)/shard_map/ppermute | solution.py:17
  17.6 2.1 %collective-permute-start.8 = (bf16[2,2,32,256]{3,2,1,0:T(8,128)(2,1)S(1)}, bf16[2,2,32,256]{3,2,1,0:T(8,128)(2,1)S(1)}, u32[]{:S(2)}, u32[]{:S(2)}) collective-permute-start(bf16[2,2,32,256]{3,2,1,0:T(8,128)(2,1)S(1)} %collective-permute-done.4.refs_0_), channel_id=1, source_target_pairs={{0,1},{1,0},{2,3},{3,2},{4,5},{5,4},{6,7},{7,6},{8,9},{9,8},{10,11... | collective-permute-start | bytes 196616 | tf_op jit(solution)/shard_map/ppermute | solution.py:17
  18.5 1.3 %collective-permute-start.9 = (bf16[2,2,32,256]{3,2,1,0:T(8,128)(2,1)S(1)}, bf16[2,2,32,256]{3,2,1,0:T(8,128)(2,1)S(1)}, u32[]{:S(2)}, u32[]{:S(2)}) collective-permute-start(bf16[2,2,32,256]{3,2,1,0:T(8,128)(2,1)S(1)} %collective-permute-done.5.refs_1_), channel_id=1, source_target_pairs={{0,1},{1,0},{2,3},{3,2},{4,5},{5,4},{6,7},{7,6},{8,9},{9,8},{10,11... | collective-permute-start | bytes 196616 | tf_op jit(solution)/shard_map/ppermute | solution.py:17
  20.9 1.5 %collective-permute-start.10 = (bf16[4,2,32,256]{3,2,1,0:T(8,128)(2,1)S(1)}, bf16[4,2,32,256]{3,2,1,0:T(8,128)(2,1)S(1)}, u32[]{:S(2)}, u32[]{:S(2)}) collective-permute-start(bf16[4,2,32,256]{3,2,1,0:T(8,128)(2,1)S(1)} %get-tuple-element.26), channel_id=1, source_target_pairs={{0,1},{1,0},{2,3},{3,2},{4,5},{5,4},{6,7},{7,6},{8,9},{9,8},{10,11... | collective-permute-start | bytes 393224 | tf_op jit(solution)/shard_map/ppermute | solution.py:17
  22.5 6.1 %collective-permute-start.11 = (bf16[2,32,256]{2,1,0:T(8,128)(2,1)S(1)}, bf16[2,32,256]{2,1,0:T(8,128)(2,1)S(1)}, u32[]{:S(2)}, u32[]{:S(2)}) collective-permute-start(bf16[2,32,256]{2,1,0:T(8,128)(2,1)S(1)} %get-tuple-element.28), channel_id=1, source_target_pairs={{0,2},{1,3},{2,4},{3,5},{4,6},{5,7},{6,0},{7,1},{8,10},{9,11},{10,... | collective-permute-start | bytes 98312 | tf_op jit(solution)/shard_map/ppermute | solution.py:22
  24.6 5.2 %collective-permute-start.12 = (bf16[2,32,256]{2,1,0:T(8,128)(2,1)S(1)}, bf16[2,32,256]{2,1,0:T(8,128)(2,1)S(1)}, u32[]{:S(2)}, u32[]{:S(2)}) collective-permute-start(bf16[2,32,256]{2,1,0:T(8,128)(2,1)S(1)} %get-tuple-element.29), channel_id=1, source_target_pairs={{0,4},{1,5},{2,6},{3,7},{4,0},{5,1},{6,2},{7,3},{8,12},{9,13},{10,... | collective-permute-start | bytes 98312 | tf_op jit(solution)/shard_map/ppermute | solution.py:22
  24.7 5.0 %collective-permute-start.13 = (bf16[2,32,256]{2,1,0:T(8,128)(2,1)S(1)}, bf16[2,32,256]{2,1,0:T(8,128)(2,1)S(1)}, u32[]{:S(2)}, u32[]{:S(2)}) collective-permute-start(bf16[2,32,256]{2,1,0:T(8,128)(2,1)S(1)} %get-tuple-element.30), channel_id=1, source_target_pairs={{0,6},{1,7},{2,0},{3,1},{4,2},{5,3},{6,4},{7,5},{8,14},{9,15},{10,... | collective-permute-start | bytes 98312 | tf_op jit(solution)/shard_map/ppermute | solution.py:22
where the time goes:
time: 30.6 us; the launch traced here: 30.4 us
  starting transfers between devices  14 us (46%)
  waiting for transfers between devices  9.45 us (31%)
  Pallas kernels  6.86 us (22%)
    ppermute x11, starting transfers between devices, swap(): return lax.ppermute(x, axis, [(i, i ^ mask) for i in range(size)])  9.5 us
    ppermute x11, waiting for transfers between devices, swap(): return lax.ppermute(x, axis, [(i, i ^ mask) for i in range(size)])  6.71 us
    ppermute x3, starting transfers between devices, along(): return lax.ppermute(x, 'term', pairs)  4.51 us
    pallas_call x7, Pallas kernels, call(): pl.pallas_call(kernel, out_shape=outs, in_specs=[pl.BlockSpec(memory_spac...  3.87 us
    pallas_call x1, Pallas kernels, direct(): pl.pallas_call(functools.partial(load_kernel, sectors), out_shape=(VMEM(l...  2.98 us
    ppermute x3, waiting for transfers between devices, along(): return lax.ppermute(x, 'term', pairs)  2.74 us
  transfers between devices with their start and end apart: 14, of which 7 were waited for; matrix products, arithmetic and copies ran while one was open for 0% of the time, Pallas kernels for 16%

commit v1 on v0

--- a/solution.py
+++ b/solution.py
@@ -97,12 +97,11 @@
 
 def apply_left(ops_ref, prod_ref, core, out_ref):
     chips, vectors, rows, states = out_ref.shape
-    total = None
-    for t in range(ops_ref.shape[0]):
-        left = jnp.concatenate(
-            [ops_ref[t, 0, pl.ds(pl.multiple_of((2 * z + core) * rows, rows), rows), :] for z in range(chips)])
-        part = jnp.dot(left, prod_ref[t], preferred_element_type=jnp.float32)
-        total = part if total is None else total + part
+    terms, states, width = prod_ref.shape
+    starts = [pl.multiple_of((2 * z + core) * rows, rows) for z in range(chips)]
+    left = jnp.concatenate([jnp.concatenate([ops_ref[t, 0, pl.ds(start, rows), :] for t in range(terms)], axis=1)
+                            for start in starts])
+    total = jnp.dot(left, prod_ref[...].reshape(terms * states, width), preferred_element_type=jnp.float32)
     for z in range(chips):
         for v in range(vectors):
             out_ref[z, v] = total[z * rows:(z + 1) * rows, v * states:(v + 1) * states].astype(out_ref.dtype)

time: 30.6 us -> 30.6 us (level)
  no operation moved by 1% of the time
where the time goes in v1:
time: 30.6 us; the launch traced here: 30.4 us
  starting transfers between devices  14 us (46%)
  waiting for transfers between devices  9.45 us (31%)
  Pallas kernels  6.86 us (22%)
    ppermute x11, starting transfers between devices, swap(): return lax.ppermute(x, axis, [(i, i ^ mask) for i in range(size)])  9.5 us
    ppermute x11, waiting for transfers between devices, swap(): return lax.ppermute(x, axis, [(i, i ^ mask) for i in range(size)])  6.71 us
    ppermute x3, starting transfers between devices, along(): return lax.ppermute(x, 'term', pairs)  4.51 us
    pallas_call x7, Pallas kernels, call(): pl.pallas_call(kernel, out_shape=outs, in_specs=[pl.BlockSpec(memory_spac...  3.87 us
    pallas_call x1, Pallas kernels, direct(): pl.pallas_call(functools.partial(load_kernel, sectors), out_shape=(VMEM(l...  2.98 us
    ppermute x3, waiting for transfers between devices, along(): return lax.ppermute(x, 'term', pairs)  2.74 us
  transfers between devices with their start and end apart: 14, of which 7 were waited for; matrix products, arithmetic and copies ran while one was open for 0% of the time, Pallas kernels for 16%

profile of v1, /device:TPU:0, one launch (start us, length us, event | category | flops | bytes accessed | tf_op | source)
XLA Modules:
  0.0 30.4 jit_solution(217160031052141375)
XLA Ops:
  0.0 3.0 %collective-permute-start = (bf16[32,1,2,256]{3,2,1,0:T(2,128)(2,1)}, bf16[32,1,2,256]{3,2,1,0:T(2,128)(2,1)S(1)}, u32[]{:S(2)}, u32[]{:S(2)}) collective-permute-start(bf16[32,1,2,256]{3,2,1,0:T(2,128)(2,1)} %wave_ref.1), channel_id=1, source_target_pairs={{0,8},{8,0},{16,24},{24,16},{1,9},{9,1},{17,25},{25,17},{2,10},{10... | collective-permute-start | bytes 98312 | tf_op jit(solution)/shard_map/ppermute | solution.py:17
  3.0 1.5 %collective-permute-start.1 = (bf16[32,1,2,256]{3,2,1,0:T(2,128)(2,1)}, bf16[32,1,2,256]{3,2,1,0:T(2,128)(2,1)S(1)}, u32[]{:S(2)}, u32[]{:S(2)}) collective-permute-start(bf16[32,1,2,256]{3,2,1,0:T(2,128)(2,1)} %wave_ref.1), channel_id=1, source_target_pairs={{0,16},{8,24},{16,0},{24,8},{1,17},{9,25},{17,1},{25,9},{2,18},{10... | collective-permute-start | bytes 98312 | tf_op jit(solution)/shard_map/ppermute | solution.py:17
  4.5 3.0 %shard_map.82 = (bf16[16,1,256,256]{3,2,1,0:T(8,128)(2,1)S(1)}, bf16[16,1,256,256]{3,2,1,0:T(8,128)(2,1)S(1)}, f32[16]{0:T(128)S(4)}, s32[16]{0:T(128)S(4)}, f32...) custom-call(s32[1,2]{1,0:T(1,128)} %coupled_ref.1, s32[4]{0:T(128)} %left_ref.1, ...), custom_call_target="tpu_custom_call" | custom-call | tf_op jit(solution)/shard_map/pallas_call | solution.py:170
  7.5 0.0 collective-permute-done.1.refs_1_
  7.5 2.0 %collective-permute-done.2.refs_2_ = bf16[32,1,2,256]{3,2,1,0:T(2,128)(2,1)S(1)} collective-permute-done((bf16[32,1,2,256]{3,2,1,0:T(2,128)(2,1)}, bf16[32,1,2,256]{3,2,1,0:T(2,128)(2,1)S(1)}, u32[]{:S(2)}, u32[]{:S(2)}) %collective-permute-start.2) | collective-permute-done | bytes 32800 | tf_op jit(solution)/shard_map/ppermute | solution.py:17
  9.5 0.1 shard_map.83.refs_0_
  9.7 3.7 %collective-permute-start.6 = (bf16[2,2,32,256]{3,2,1,0:T(8,128)(2,1)S(1)}, bf16[2,2,32,256]{3,2,1,0:T(8,128)(2,1)S(1)}, u32[]{:S(2)}, u32[]{:S(2)}) collective-permute-start(bf16[2,2,32,256]{3,2,1,0:T(8,128)(2,1)S(1)} %shard_map.83.refs_0_), channel_id=1, source_target_pairs={{0,6},{1,7},{2,4},{3,5},{4,2},{5,3},{6,0},{7,1},{8,14},{9,15},{10,... | collective-permute-start | bytes 196616 | tf_op jit(solution)/shard_map/ppermute | solution.py:17
  13.3 0.8 %collective-permute-start.5 = (bf16[2,2,32,256]{3,2,1,0:T(8,128)(2,1)S(1)}, bf16[2,2,32,256]{3,2,1,0:T(8,128)(2,1)S(1)}, u32[]{:S(2)}, u32[]{:S(2)}) collective-permute-start(bf16[2,2,32,256]{3,2,1,0:T(8,128)(2,1)S(1)} %shard_map.83.refs_0_), channel_id=1, source_target_pairs={{0,4},{1,5},{2,6},{3,7},{4,0},{5,1},{6,2},{7,3},{8,12},{9,13},{10,... | collective-permute-start | bytes 196616 | tf_op jit(solution)/shard_map/ppermute | solution.py:17
  14.1 1.8 %collective-permute-done.6.refs_2_ = bf16[2,2,32,256]{3,2,1,0:T(8,128)(2,1)S(1)} collective-permute-done((bf16[2,2,32,256]{3,2,1,0:T(8,128)(2,1)S(1)}, bf16[2,2,32,256]{3,2,1,0:T(8,128)(2,1)S(1)}, u32[]{:S(2)}, u32[]{:S(2)}) %collective-permute-start.6) | collective-permute-done | bytes 65568 | tf_op jit(solution)/shard_map/ppermute | solution.py:17
  15.9 1.7 %collective-permute-done.4.refs_0_ = bf16[2,2,32,256]{3,2,1,0:T(8,128)(2,1)S(1)} collective-permute-done((bf16[2,2,32,256]{3,2,1,0:T(8,128)(2,1)S(1)}, bf16[2,2,32,256]{3,2,1,0:T(8,128)(2,1)S(1)}, u32[]{:S(2)}, u32[]{:S(2)}) %collective-permute-start.4) | collective-permute-done | bytes 65568 | tf_op jit(solution)/shard_map/ppermute | solution.py:17
  17.6 0.9 %collective-permute-done.5.refs_1_ = bf16[2,2,32,256]{3,2,1,0:T(8,128)(2,1)S(1)} collective-permute-done((bf16[2,2,32,256]{3,2,1,0:T(8,128)(2,1)S(1)}, bf16[2,2,32,256]{3,2,1,0:T(8,128)(2,1)S(1)}, u32[]{:S(2)}, u32[]{:S(2)}) %collective-permute-start.5) | collective-permute-done | bytes 65568 | tf_op jit(solution)/shard_map/ppermute | solution.py:17
  18.5 0.5 %shard_map.84.prod_in = bf16[16,256,512]{2,1,0:T(8,128)(2,1)S(1)} custom-call(f32[16]{0:T(128)S(4)} %get-tuple-element.20.scale_ref, s32[16]{0:T(128)S(4)} %get-tuple-element.21.source_ref, bf16[16,1,256,256]{3,2,1,0:T(8,128)(2,1)S(1)} %get-tuple-element.22.coops_ref, bf16[2,2,32,256]{3,2,1,0:T(8,128)(2,1)S(1)} %shard_map.83.refs_0_, ...), custom_call_target="tpu_custom_call" | custom-call | tf_op jit(solution)/shard_map/pallas_call | solution.py:139
  19.0 0.7 %shard_map.85.prod_in = bf16[16,256,512]{2,1,0:T(8,128)(2,1)S(1)} custom-call(f32[16]{0:T(128)S(4)} %get-tuple-element.20.scale_ref, s32[16]{0:T(128)S(4)} %get-tuple-element.21.source_ref, bf16[16,1,256,256]{3,2,1,0:T(8,128)(2,1)S(1)} %get-tuple-element.22.coops_ref, bf16[16,256,512]{2,1,0:T(8,128)(2,1)S(1)} %shard_map.84.prod_in, ...), custom_call_target="tpu_custom_call", output_to_operand_aliasing={{}: (3, {})} | custom-call | tf_op jit(solution)/shard_map/pallas_call | solution.py:139
  19.7 0.0 collective-permute-done.9.refs_1_
  19.7 1.2 %shard_map.86 = (bf16[16,256,512]{2,1,0:T(8,128)(2,1)S(1)}, bf16[4,2,32,256]{3,2,1,0:T(8,128)(2,1)S(1)}) custom-call(f32[16]{0:T(128)S(4)} %get-tuple-element.20.scale_ref, s32[16]{0:T(128)S(4)} %get-tuple-element.21.source_ref, bf16[16,1,256,256]{3,2,1,0:T(8,128)(2,1)S(1)} %get-tuple-element.22.coops_ref, ...), custom_call_target="tpu_custom_call", output_to_operand_aliasing={{0}: (4, {})} | custom-call | tf_op jit(solution)/shard_map/pallas_call | solution.py:139
  20.9 0.6 %collective-permute-start.10 = (bf16[4,2,32,256]{3,2,1,0:T(8,128)(2,1)S(1)}, bf16[4,2,32,256]{3,2,1,0:T(8,128)(2,1)S(1)}, u32[]{:S(2)}, u32[]{:S(2)}) collective-permute-start(bf16[4,2,32,256]{3,2,1,0:T(8,128)(2,1)S(1)} %get-tuple-element.26), channel_id=1, source_target_pairs={{0,1},{1,0},{2,3},{3,2},{4,5},{5,4},{6,7},{7,6},{8,9},{9,8},{10,11... | collective-permute-start | bytes 393224 | tf_op jit(solution)/shard_map/ppermute | solution.py:17
  21.5 0.7 %shard_map.87.keep_ref = f32[4,2,32,256]{3,2,1,0:T(8,128)S(1)} custom-call(bf16[16,1,256,256]{3,2,1,0:T(8,128)(2,1)S(1)} %get-tuple-element.19.ops_ref, bf16[16,256,512]{2,1,0:T(8,128)(2,1)S(1)} %get-tuple-element.25.prod_ref), custom_call_target="tpu_custom_call" | custom-call | tf_op jit(solution)/shard_map/pallas_call | solution.py:139
  22.2 0.3 collective-permute-done.10.recv_ref
  22.5 2.1 %collective-permute-start.11 = (bf16[2,32,256]{2,1,0:T(8,128)(2,1)S(1)}, bf16[2,32,256]{2,1,0:T(8,128)(2,1)S(1)}, u32[]{:S(2)}, u32[]{:S(2)}) collective-permute-start(bf16[2,32,256]{2,1,0:T(8,128)(2,1)S(1)} %get-tuple-element.28), channel_id=1, source_target_pairs={{0,2},{1,3},{2,4},{3,5},{4,6},{5,7},{6,0},{7,1},{8,10},{9,11},{10,... | collective-permute-start | bytes 98312 | tf_op jit(solution)/shard_map/ppermute | solution.py:22
  24.6 0.1 collective-permute-start.12
  24.7 2.3 %collective-permute-start.13 = (bf16[2,32,256]{2,1,0:T(8,128)(2,1)S(1)}, bf16[2,32,256]{2,1,0:T(8,128)(2,1)S(1)}, u32[]{:S(2)}, u32[]{:S(2)}) collective-permute-start(bf16[2,32,256]{2,1,0:T(8,128)(2,1)S(1)} %get-tuple-element.30), channel_id=1, source_target_pairs={{0,6},{1,7},{2,0},{3,1},{4,2},{5,3},{6,4},{7,5},{8,14},{9,15},{10,... | collective-permute-start | bytes 98312 | tf_op jit(solution)/shard_map/ppermute | solution.py:22
  27.0 1.6 %collective-permute-done.11.refs_0_ = bf16[2,32,256]{2,1,0:T(8,128)(2,1)S(1)} collective-permute-done((bf16[2,32,256]{2,1,0:T(8,128)(2,1)S(1)}, bf16[2,32,256]{2,1,0:T(8,128)(2,1)S(1)}, u32[]{:S(2)}, u32[]{:S(2)}) %collective-permute-start.11) | collective-permute-done | bytes 32800 | tf_op jit(solution)/shard_map/ppermute | solution.py:22
  28.6 1.1 %collective-permute-done.12.refs_1_ = bf16[2,32,256]{2,1,0:T(8,128)(2,1)S(1)} collective-permute-done((bf16[2,32,256]{2,1,0:T(8,128)(2,1)S(1)}, bf16[2,32,256]{2,1,0:T(8,128)(2,1)S(1)}, u32[]{:S(2)}, u32[]{:S(2)}) %collective-permute-start.12) | collective-permute-done | bytes 32800 | tf_op jit(solution)/shard_map/ppermute | solution.py:22
  29.7 0.7 %shard_map.89 = bf16[32,1,2,256]{3,2,1,0:T(2,128)(2,1)} custom-call(f32[32,256]{1,0:T(8,128)S(1)} %get-tuple-element.18.live_ref, f32[2,32,256]{2,1,0:T(8,128)S(1)} %get-tuple-element.27.total_ref, bf16[2,32,256]{2,1,0:T(8,128)(2,1)S(1)} %collective-permute-done.11.refs_0_, bf16[2,32,256]{2,1,0:T(8,128)(2,1)S(1)} %collective-permute-done.12.refs_1_, ...), custom_call_target="tpu_custom_call" | custom-call | tf_op jit(solution)/shard_map/pallas_call | solution.py:139
  (12 shorter events, 0.1 us)
Async XLA Ops:
  0.0 7.5 %collective-permute-start = (bf16[32,1,2,256]{3,2,1,0:T(2,128)(2,1)}, bf16[32,1,2,256]{3,2,1,0:T(2,128)(2,1)S(1)}, u32[]{:S(2)}, u32[]{:S(2)}) collective-permute-start(bf16[32,1,2,256]{3,2,1,0:T(2,128)(2,1)} %wave_ref.1), channel_id=1, source_target_pairs={{0,8},{8,0},{16,24},{24,16},{1,9},{9,1},{17,25},{25,17},{2,10},{10... | collective-permute-start | bytes 98312 | tf_op jit(solution)/shard_map/ppermute | solution.py:17
  3.0 4.5 %collective-permute-start.1 = (bf16[32,1,2,256]{3,2,1,0:T(2,128)(2,1)}, bf16[32,1,2,256]{3,2,1,0:T(2,128)(2,1)S(1)}, u32[]{:S(2)}, u32[]{:S(2)}) collective-permute-start(bf16[32,1,2,256]{3,2,1,0:T(2,128)(2,1)} %wave_ref.1), channel_id=1, source_target_pairs={{0,16},{8,24},{16,0},{24,8},{1,17},{9,25},{17,1},{25,9},{2,18},{10... | collective-permute-start | bytes 98312 | tf_op jit(solution)/shard_map/ppermute | solution.py:17
  4.5 5.0 %collective-permute-start.2 = (bf16[32,1,2,256]{3,2,1,0:T(2,128)(2,1)}, bf16[32,1,2,256]{3,2,1,0:T(2,128)(2,1)S(1)}, u32[]{:S(2)}, u32[]{:S(2)}) collective-permute-start(bf16[32,1,2,256]{3,2,1,0:T(2,128)(2,1)} %wave_ref.1), channel_id=1, source_target_pairs={{0,24},{8,16},{16,8},{24,0},{1,25},{9,17},{17,9},{25,1},{2,26},{10... | collective-permute-start | bytes 98312 | tf_op jit(solution)/shard_map/ppermute | solution.py:17
  9.7 6.2 %collective-permute-start.6 = (bf16[2,2,32,256]{3,2,1,0:T(8,128)(2,1)S(1)}, bf16[2,2,32,256]{3,2,1,0:T(8,128)(2,1)S(1)}, u32[]{:S(2)}, u32[]{:S(2)}) collective-permute-start(bf16[2,2,32,256]{3,2,1,0:T(8,128)(2,1)S(1)} %shard_map.83.refs_0_), channel_id=1, source_target_pairs={{0,6},{1,7},{2,4},{3,5},{4,2},{5,3},{6,0},{7,1},{8,14},{9,15},{10,... | collective-permute-start | bytes 196616 | tf_op jit(solution)/shard_map/ppermute | solution.py:17
  13.3 4.3 %collective-permute-start.4 = (bf16[2,2,32,256]{3,2,1,0:T(8,128)(2,1)S(1)}, bf16[2,2,32,256]{3,2,1,0:T(8,128)(2,1)S(1)}, u32[]{:S(2)}, u32[]{:S(2)}) collective-permute-start(bf16[2,2,32,256]{3,2,1,0:T(8,128)(2,1)S(1)} %shard_map.83.refs_0_), channel_id=1, source_target_pairs={{0,2},{1,3},{2,0},{3,1},{4,6},{5,7},{6,4},{7,5},{8,10},{9,11},{10,... | collective-permute-start | bytes 196616 | tf_op jit(solution)/shard_map/ppermute | solution.py:17
  13.3 5.2 %collective-permute-start.5 = (bf16[2,2,32,256]{3,2,1,0:T(8,128)(2,1)S(1)}, bf16[2,2,32,256]{3,2,1,0:T(8,128)(2,1)S(1)}, u32[]{:S(2)}, u32[]{:S(2)}) collective-permute-start(bf16[2,2,32,256]{3,2,1,0:T(8,128)(2,1)S(1)} %shard_map.83.refs_0_), channel_id=1, source_target_pairs={{0,4},{1,5},{2,6},{3,7},{4,0},{5,1},{6,2},{7,3},{8,12},{9,13},{10,... | collective-permute-start | bytes 196616 | tf_op jit(solution)/shard_map/ppermute | solution.py:17
  14.1 4.4 %collective-permute-start.3 = (bf16[2,2,32,256]{3,2,1,0:T(8,128)(2,1)S(1)}, bf16[2,2,32,256]{3,2,1,0:T(8,128)(2,1)S(1)}, u32[]{:S(2)}, u32[]{:S(2)}) collective-permute-start(bf16[2,2,32,256]{3,2,1,0:T(8,128)(2,1)S(1)} %shard_map.83.refs_0_), channel_id=1, source_target_pairs={{0,1},{1,0},{2,3},{3,2},{4,5},{5,4},{6,7},{7,6},{8,9},{9,8},{10,11... | collective-permute-start | bytes 196616 | tf_op jit(solution)/shard_map/ppermute | solution.py:17
  15.9 3.1 %collective-permute-start.7 = (bf16[2,2,32,256]{3,2,1,0:T(8,128)(2,1)S(1)}, bf16[2,2,32,256]{3,2,1,0:T(8,128)(2,1)S(1)}, u32[]{:S(2)}, u32[]{:S(2)}) collective-permute-start(bf16[2,2,32,256]{3,2,1,0:T(8,128)(2,1)S(1)} %collective-permute-done.6.refs_2_), channel_id=1, source_target_pairs={{0,1},{1,0},{2,3},{3,2},{4,5},{5,4},{6,7},{7,6},{8,9},{9,8},{10,11... | collective-permute-start | bytes 196616 | tf_op jit(solution)/shard_map/ppermute | solution.py:17
  17.6 2.1 %collective-permute-start.8 = (bf16[2,2,32,256]{3,2,1,0:T(8,128)(2,1)S(1)}, bf16[2,2,32,256]{3,2,1,0:T(8,128)(2,1)S(1)}, u32[]{:S(2)}, u32[]{:S(2)}) collective-permute-start(bf16[2,2,32,256]{3,2,1,0:T(8,128)(2,1)S(1)} %collective-permute-done.4.refs_0_), channel_id=1, source_target_pairs={{0,1},{1,0},{2,3},{3,2},{4,5},{5,4},{6,7},{7,6},{8,9},{9,8},{10,11... | collective-permute-start | bytes 196616 | tf_op jit(solution)/shard_map/ppermute | solution.py:17
  18.5 1.3 %collective-permute-start.9 = (bf16[2,2,32,256]{3,2,1,0:T(8,128)(2,1)S(1)}, bf16[2,2,32,256]{3,2,1,0:T(8,128)(2,1)S(1)}, u32[]{:S(2)}, u32[]{:S(2)}) collective-permute-start(bf16[2,2,32,256]{3,2,1,0:T(8,128)(2,1)S(1)} %collective-permute-done.5.refs_1_), channel_id=1, source_target_pairs={{0,1},{1,0},{2,3},{3,2},{4,5},{5,4},{6,7},{7,6},{8,9},{9,8},{10,11... | collective-permute-start | bytes 196616 | tf_op jit(solution)/shard_map/ppermute | solution.py:17
  20.9 1.5 %collective-permute-start.10 = (bf16[4,2,32,256]{3,2,1,0:T(8,128)(2,1)S(1)}, bf16[4,2,32,256]{3,2,1,0:T(8,128)(2,1)S(1)}, u32[]{:S(2)}, u32[]{:S(2)}) collective-permute-start(bf16[4,2,32,256]{3,2,1,0:T(8,128)(2,1)S(1)} %get-tuple-element.26), channel_id=1, source_target_pairs={{0,1},{1,0},{2,3},{3,2},{4,5},{5,4},{6,7},{7,6},{8,9},{9,8},{10,11... | collective-permute-start | bytes 393224 | tf_op jit(solution)/shard_map/ppermute | solution.py:17
  22.5 6.1 %collective-permute-start.11 = (bf16[2,32,256]{2,1,0:T(8,128)(2,1)S(1)}, bf16[2,32,256]{2,1,0:T(8,128)(2,1)S(1)}, u32[]{:S(2)}, u32[]{:S(2)}) collective-permute-start(bf16[2,32,256]{2,1,0:T(8,128)(2,1)S(1)} %get-tuple-element.28), channel_id=1, source_target_pairs={{0,2},{1,3},{2,4},{3,5},{4,6},{5,7},{6,0},{7,1},{8,10},{9,11},{10,... | collective-permute-start | bytes 98312 | tf_op jit(solution)/shard_map/ppermute | solution.py:22
  24.6 5.2 %collective-permute-start.12 = (bf16[2,32,256]{2,1,0:T(8,128)(2,1)S(1)}, bf16[2,32,256]{2,1,0:T(8,128)(2,1)S(1)}, u32[]{:S(2)}, u32[]{:S(2)}) collective-permute-start(bf16[2,32,256]{2,1,0:T(8,128)(2,1)S(1)} %get-tuple-element.29), channel_id=1, source_target_pairs={{0,4},{1,5},{2,6},{3,7},{4,0},{5,1},{6,2},{7,3},{8,12},{9,13},{10,... | collective-permute-start | bytes 98312 | tf_op jit(solution)/shard_map/ppermute | solution.py:22
  24.7 5.0 %collective-permute-start.13 = (bf16[2,32,256]{2,1,0:T(8,128)(2,1)S(1)}, bf16[2,32,256]{2,1,0:T(8,128)(2,1)S(1)}, u32[]{:S(2)}, u32[]{:S(2)}) collective-permute-start(bf16[2,32,256]{2,1,0:T(8,128)(2,1)S(1)} %get-tuple-element.30), channel_id=1, source_target_pairs={{0,6},{1,7},{2,0},{3,1},{4,2},{5,3},{6,4},{7,5},{8,14},{9,15},{10,... | collective-permute-start | bytes 98312 | tf_op jit(solution)/shard_map/ppermute | solution.py:22
